TPU v7x, 512 devices: a whole 4x4x16 slice. The times are simulated.
512 devices in a mesh: param: 8 (over x, core), feat: 16 (over z), ex: 4 (over y).
Axes of the slice: x: 4, y: 4, z: 16, core: 2. Of those that a mesh axis runs over, the one named last changes fastest.
Arguments:
- gradients: float32 [2048, 8192], P('ex', 'param'), may hold values from -6 to 6
- projection: float32 [8192, 4, 16, 256], P('param', None, 'feat'), may hold values from -0.0625 to 0.0625
- factor: float32 [4, 16, 256, 1024], P(None, 'feat', 'param'), may hold values from -0.1875 to 0.1875
- diag_inverse: float32 [4, 256, 256], P(None, 'param'), may hold values from -1 to 1.5, as said below
- queries: float32 [4, 16, 256, 256], P(None, 'feat', 'param', 'ex'), may hold values from -6 to 6
Outputs:
- scores: float32 [256, 2048], P('param', 'ex')
- trailing: float32 [4, 16, 256, 2048], P(None, 'feat', 'param', 'ex')
- trailing_queries: float32 [4, 16, 256, 256], P(None, 'feat', 'param', 'ex')
Inputs may be any that keep to these rules, and one draw needn't show every extreme that they name: `diag_inverse`: every block is upper triangular, with diagonal entries of 0.5 to 1.5.
All inputs are finite; a program needn't handle non-finite values.
Results may differ from a plain program's by a relative error of at most 0.00017.
Values sent between devices are 32-bit elements; how exact they have to be, the bound alone decides.
A program may use at most 128 MiB of HBM per device.

v0:
```python
import math

import jax
import jax.numpy as jnp
from jax import lax
from jax.sharding import PartitionSpec as P

exact_mode = lax.Precision.HIGHEST


def sent_together(arrays, axis, dim, along):
    both = jnp.concatenate(arrays, axis=along)
    filled, at, gathered = (lax.all_gather(both, axis, axis=dim, tiled=True), 0, [])
    for a in arrays:
        gathered.append(lax.slice_in_dim(filled, at, at + a.shape[along], axis=along))
        at += a.shape[along]
    return tuple(gathered)


def joined_along(blocks, dim):
    blocks = jnp.moveaxis(blocks, 0, dim)
    shape = blocks.shape
    return blocks.reshape(*shape[:dim], shape[dim] * shape[dim + 1], *shape[dim + 2 :])


def sent_to_all(x, axis):
    peers = lax.axis_size(axis)
    return lax.all_to_all(jnp.broadcast_to(x[None], (peers, *x.shape)), axis, 0, 0, tiled=True)


def collect(x, axis, dim):
    return joined_along(sent_to_all(x, axis), dim)


def per_device(gradients, projection, factor, diag_inverse, queries):
    feat_count = lax.axis_size("feat")
    param_count = lax.axis_size("param")
    rounds = projection.shape[1]
    panel_size = projection.shape[3]
    ex_rows = gradients.shape[0]
    panel_total = diag_inverse.shape[0]
    weights = projection[:, :, 0, :]
    projected = lax.psum_scatter(
        jnp.einsum("ep,pmr->rme", gradients, weights, precision=exact_mode),
        "param",
        scatter_dimension=0,
        tiled=True,
    )
    right_sides = jnp.concatenate([jnp.transpose(projected, (1, 0, 2)), queries[:, 0]], axis=2)
    factor_rows = factor[:, 0]
    feat_place = lax.axis_index("feat")
    panel_order = jnp.arange(rounds) * feat_count + feat_place
    solved_list = []
    held_rows = []
    held_factor = []
    for panel_index in range(panel_total):
        owner_here = feat_place == panel_index % feat_count
        round_index = panel_index // feat_count
        held_rows.append(jnp.where(owner_here, right_sides[round_index], 0.0))
        held_factor.append(jnp.where(owner_here, factor_rows[round_index], 0.0))
    summed_rows, summed_factor = lax.psum((jnp.stack(held_rows), jnp.stack(held_factor)), "feat")
    whole_rows, whole_factor, whole_inverse = sent_together(
        (summed_rows, summed_factor, diag_inverse), "param", 1, 2
    )
    for panel_index in range(panel_total):
        pending = whole_rows[panel_index]
        for earlier in range(panel_index):
            block = whole_factor[panel_index][:, earlier * panel_size : (earlier + 1) * panel_size]
            pending = pending - jnp.dot(block, solved_list[earlier], precision=exact_mode)
        solved_list.append(
            jnp.einsum("kr,kc->rc", whole_inverse[panel_index], pending, precision=exact_mode)
        )
    for panel_index in range(panel_total):
        solved = solved_list[panel_index]
        apply_columns = factor_rows[:, :, panel_index * panel_size : (panel_index + 1) * panel_size]
        update = jnp.einsum("mrk,kc->mrc", apply_columns, solved, precision=exact_mode)
        right_sides = jnp.where(
            (panel_order > panel_index)[:, None, None], right_sides - update, right_sides
        )
    window = jnp.concatenate(solved_list, axis=0)
    train_part = window[:, :ex_rows]
    query_part = collect(window[:, ex_rows:], "ex", 1)
    slice_width = query_part.shape[1] // param_count
    own_queries = lax.dynamic_slice_in_dim(
        query_part, lax.axis_index("param") * slice_width, slice_width, 1
    )
    scores = jnp.einsum("kq,ke->qe", own_queries, train_part, precision=exact_mode) / math.sqrt(
        window.shape[0]
    )
    trailing = right_sides[:, None, :, :ex_rows]
    trailing_queries = right_sides[:, None, :, ex_rows:]
    return (scores, trailing, trailing_queries)


def solution(mesh):
    return jax.shard_map(
        per_device,
        mesh=mesh,
        in_specs=(
            P("ex", "param"),
            P("param", None, "feat", None),
            P(None, "feat", "param", None),
            P(None, "param", None),
            P(None, "feat", "param", "ex"),
        ),
        out_specs=(
            P("param", "ex"),
            P(None, "feat", "param", "ex"),
            P(None, "feat", "param", "ex"),
        ),
        check_vma=False,
    )
```

profile of v0, /device:TPU:1, one launch (start us, length us, event | category | flops | bytes accessed | tf_op | source)
XLA Modules:
  0.0 321.8 jit_solution(12311713182572855918)
XLA Ops:
  7.2 11.1 %copy.15 = f32[1024,4,1,256]{0,3,1,2:T(8,128)} copy(f32[1024,4,1,256]{3,2,1,0:T(1,128)} %param.6) | data formatting | bytes 8388608 | tf_op jit(solution)/shard_map/squeeze | solution.py:42
  18.3 9.9 %fusion.5 = f32[256,4,512]{2,0,1:T(8,128)} fusion(f32[512,1024]{1,0:T(8,128)S(1)} %copy-done, f32[1024,4,1,256]{0,3,1,2:T(8,128)} %copy.15), kind=kOutput, calls=%fused_computation.8 | convolution fusion | flops 6442450944 | bytes 8388608 | tf_op jit(solution)/shard_map/ep,pmr->rme/dot_general | solution.py:44
  28.3 1.0 select_bitcast_fusion.3
  30.1 43.4 %reduce-scatter.2.cloned.1.call-done = f32[32,4,512]{2,0,1:T(8,128)} async-done(((f32[256,4,512]{2,0,1:T(8,128)}), f32[32,4,512]{2,0,1:T(8,128)}) %reduce-scatter.2.cloned.1.call-update) | async-done | bytes 262160 | tf_op jit(solution)/shard_map/reduce_scatter | solution.py:43
  73.5 0.9 broadcast_select_fusion.3
  75.4 130.5 %all-reduce.3.cloned.1.call-done = (f32[4,32,576]{2,1,0:T(8,128)}, f32[4,32,1024]{2,1,0:T(8,128)}) async-done(((f32[4,32,576]{2,1,0:T(8,128)}, f32[4,32,1024]{2,1,0:T(8,128)}), (f32[4,32,576]{2,1,0:T(8,128)}, f32[4,32,1024]{2,1,0:T(8,128)})) %all-reduce.3.cloned.1.call-update) | async-done | bytes 819216 | tf_op jit(solution)/shard_map/psum | solution.py:61
  205.9 2.4 concatenate.10
  208.4 61.5 %all-gather.2.cloned.1.call-done = f32[4,256,1856]{2,1,0:T(8,128)} async-done(((f32[4,32,1856]{2,1,0:T(8,128)}), f32[4,256,1856]{2,1,0:T(8,128)}) %all-gather.2.cloned.1.call-update) | async-done | bytes 7602192 | tf_op jit(solution)/shard_map/all_gather | solution.py:13
  269.9 2.5 fusion.19
  272.4 2.9 slice_bitcast_fusion.1
  275.2 1.9 convolution_subtract_fusion.5
  277.1 2.3 fusion.32
  279.4 1.9 convolution_subtract_fusion.4
  282.1 1.9 convolution_subtract_fusion.2
  284.8 2.3 fusion.30
  287.9 2.3 fusion.27
  291.1 1.1 broadcast_in_dim.55
  292.2 4.5 %all-to-all-start = ((f32[4,1024,64]{1,2,0:T(8,128)}), f32[4,1024,64]{1,2,0:T(8,128)}, u32[]{:S(2)}, u32[]{:S(2)}) async-start(f32[4,1024,64]{1,2,0:T(8,128)} %broadcast_in_dim.55), calls=%async_computation.1 | async-start | bytes 2097152 | tf_op jit(solution)/shard_map/all_to_all | solution.py:28
  296.7 1.7 fusion.17
  298.4 1.7 fusion.15
  300.1 1.8 fusion.13
  301.9 1.7 fusion.11
  304.9 6.4 %all-to-all-done = f32[4,1024,64]{1,2,0:T(8,128)} async-done(((f32[4,1024,64]{1,2,0:T(8,128)}), f32[4,1024,64]{1,2,0:T(8,128)}, u32[]{:S(2)}, u32[]{:S(2)}) %all-to-all-start) | async-done | bytes 1048608 | tf_op jit(solution)/shard_map/all_to_all | solution.py:28
  311.4 3.9 %fusion.18 = f32[32,512]{1,0:T(8,128)} fusion(f32[256,576]{0,1:T(8,128)} %copy-done.2, f32[256,576]{0,1:T(8,128)} %copy-done.1, f32[256,576]{0,1:T(8,128)S(1)} %fusion.32, f32[256,576]{0,1:T(8,128)S(1)} %fusion.19, f32[1024,256]{0,1:T(8,128)} %bitcast.21, s32[]{:T(128)S(6)} %select_n.132), kind=kOutput, calls=%fused_computation.27 | convolution fusion | flops 202915840 | bytes 2555908 | tf_op jit(solution)/shard_map/kq,ke->qe/dot_general | solution.py:87
  (31 shorter events, 6.6 us)
Async XLA Ops:
  7.2 11.1 %copy-start = (f32[512,1024]{1,0:T(8,128)S(1)}, f32[512,1024]{1,0:T(8,128)}, u32[]{:S(2)}) copy-start(f32[512,1024]{1,0:T(8,128)} %param.5) | copy-start | bytes 6291460
  7.2 66.3 %reduce-scatter.2.cloned.1.call-start = ((), (), s32[]{:S(2)}) async-start(), calls=%async_computation.2 | async-start | bytes 2359296 | tf_op jit(solution)/shard_map/reduce_scatter | solution.py:43
  18.3 55.2 %copy-start.5 = (f32[4,1,32,64]{3,2,1,0:T(8,128)S(1)}, f32[4,1,32,64]{3,2,1,0:T(8,128)}, u32[]{:S(2)}) copy-start(f32[4,1,32,64]{3,2,1,0:T(8,128)} %param.9) | copy-start | bytes 98308
  28.2 177.7 %copy-start.6 = (f32[4,32,256]{2,1,0:T(8,128)S(1)}, f32[4,32,256]{2,1,0:T(8,128)}, u32[]{:S(2)}) copy-start(f32[4,32,256]{2,1,0:T(8,128)} %param.8) | copy-start | bytes 393220
  28.3 177.6 %all-reduce.3.cloned.1.call-start = ((), (), s32[]{:S(2)}) async-start(), calls=%async_computation.4 | async-start | bytes 1703936 | tf_op jit(solution)/shard_map/psum | solution.py:61
  75.2 194.7 %all-gather.2.cloned.1.call-start = ((), (), s32[]{:S(2)}) async-start(), calls=%async_computation.3 | async-start | bytes 8847360 | tf_op jit(solution)/shard_map/all_gather | solution.py:13
  287.1 3.2 copy-start.1
  287.9 8.7 %copy-start.4 = (f32[32,4,512]{2,0,1:T(8,128)S(1)}, f32[32,4,512]{2,0,1:T(8,128)}, u32[]{:S(2)}) copy-start(f32[32,4,512]{2,0,1:T(8,128)} %reduce-scatter.2.cloned.1.call-done) | copy-start | bytes 786436
  290.3 0.8 copy-start.2
  292.2 19.2 %all-to-all-start = ((f32[4,1024,64]{1,2,0:T(8,128)}), f32[4,1024,64]{1,2,0:T(8,128)}, u32[]{:S(2)}, u32[]{:S(2)}) async-start(f32[4,1024,64]{1,2,0:T(8,128)} %broadcast_in_dim.55), calls=%async_computation.1 | async-start | bytes 2097152 | tf_op jit(solution)/shard_map/all_to_all | solution.py:28
  296.7 5.2 %copy-start.3 = (f32[256,576]{0,1:T(8,128)S(1)}, f32[256,576]{0,1:T(8,128)}, u32[]{:S(2)}) copy-start(f32[256,576]{0,1:T(8,128)} %copy-done.2) | copy-start | bytes 1769476
Sparse Core Ops, SparseCore 0:
  28.4 45.0 reduce-scatter.1
  75.9 129.9 all-reduce.2
  208.5 61.3 all-gather.1
where the time goes:
time: 323 us; the launch traced here: 322 us
  waiting for transfers between devices  242 us (75%)
  matrix products  38.1 us (12%)
  local copies, waits for them, and re-layouts  19.6 us (6%)
  between operations  14 us (4%)
  starting transfers between devices  4.77 us (1%)
  other arithmetic  3.45 us (1%)
    psum x1, waiting for transfers between devices, per_device(): lax.psum((jnp.stack(held_rows), jnp.stack(held_factor)), 'feat')  131 us
    all_gather x1, waiting for transfers between devices, sent_together(): lax.all_gather(both, axis, axis=dim, tiled=True)  61.5 us
    reduce_scatter x1, waiting for transfers between devices, per_device(): lax.psum_scatter(jnp.einsum('ep,pmr->rme', gradients, weights, precision=...  43.4 us
    squeeze x1, local copies, waits for them, and re-layouts, per_device(): weights = projection[:, :, 0, :]  11.1 us
    dot_general x1, matrix products, per_device(): jnp.einsum('ep,pmr->rme', gradients, weights, precision=exact_mode)  9.94 us
    dot_general x4, matrix products, per_device(): jnp.einsum('kr,kc->rc', whole_inverse[panel_index], pending, precision=ex...  9.34 us
    dot_general x6, matrix products, per_device(): jnp.dot(block, solved_list[earlier], precision=exact_mode)  8.08 us
    dot_general x4, matrix products, per_device(): jnp.einsum('mrk,kc->mrc', apply_columns, solved, precision=exact_mode)  6.87 us
  transfers between devices with their start and end apart: 4, of which 4 were waited for; matrix products, arithmetic and copies ran while one was open for 3% of the time, Pallas kernels for 0%

commit v1 on v0

v1 whole, which is shorter than its diff:
```python
import math

import jax
import jax.numpy as jnp
from jax import lax
from jax.experimental import pallas as pl
from jax.experimental.pallas import tpu as pltpu
from jax.sharding import PartitionSpec as P

MESH = pl.DeviceIdType.MESH
F32 = jnp.float32
BF16 = jnp.bfloat16
CHIPS = 4
PANELS = 4
RING = 16
UP = 8
KP = 256


def halves(x):
    hi = x.astype(BF16)
    return hi, (x - hi.astype(F32)).astype(BF16)


def left3(x, axis):
    hi, lo = halves(x)
    return jnp.concatenate([hi, lo, hi], axis=axis)


def right3(x, axis):
    hi, lo = halves(x)
    return jnp.concatenate([hi, hi, lo], axis=axis)


def dot_nn(a, b):
    return jnp.dot(left3(a, 1), right3(b, 0), preferred_element_type=F32)


def dot_nt(a, b):
    return lax.dot_general(
        left3(a, 1), right3(b, 1), (((1,), (1,)), ((), ())), preferred_element_type=F32
    )


class Place:
    def __init__(self):
        self.p = lax.axis_index("param")
        self.z = lax.axis_index("feat")
        self.y = lax.axis_index("ex")
        self.x = lax.div(self.p, 2)
        self.c = lax.rem(self.p, 2)
        self.xp = lax.rem(self.x + 1, CHIPS)
        self.xm = lax.rem(self.x + CHIPS - 1, CHIPS)
        self.xo = lax.rem(self.x + 2, CHIPS)
        self.right = {"param": 2 * self.xp + self.c}
        self.left = {"param": 2 * self.xm + self.c}
        self.sib = {"param": 2 * self.x + 1 - self.c}
        self.above = {"feat": lax.rem(self.z + 1, RING)}
        self.below = {"feat": lax.rem(self.z + RING - 1, RING)}

    def slot(self, x, c):
        return 2 * x + c


def rdma(src, dst, ss, rs, dev):
    return pltpu.make_async_remote_copy(
        src_ref=src, dst_ref=dst, send_sem=ss, recv_sem=rs, device_id=dev, device_id_type=MESH
    )


class Gather:
    def __init__(self, pos, chunk, half_a, half_b, ss, rs):
        self.pos, self.chunk, self.half_a, self.half_b, self.ss, self.rs = pos, chunk, half_a, half_b, ss, rs
        q = pos
        self.own = q.slot(q.x, q.c)
        self.i_m = q.slot(q.xm, q.c)
        self.i_p = q.slot(q.xp, q.c)
        self.i_o = q.slot(q.xo, q.c)

    def copy(self, k):
        q = self.pos
        ref, dev = (
            lambda: (self.chunk(self.own), q.right),
            lambda: (self.chunk(self.own), q.left),
            lambda: (self.half_a(self.i_m), q.right),
            lambda: (self.half_b(self.i_p), q.left),
            lambda: (self.chunk(self.own), q.sib),
            lambda: (self.chunk(self.i_m), q.sib),
            lambda: (self.chunk(self.i_p), q.sib),
            lambda: (self.chunk(self.i_o), q.sib),
        )[k]()
        return rdma(ref, ref, self.ss.at[k], self.rs.at[k], dev)

    def arrive(self, ref, k):
        rdma(ref, ref, self.ss.at[k], self.rs.at[k], self.pos.sib).wait_recv()

    def start(self):
        for k in (0, 1, 4):
            self.copy(k).start()

    def mid(self):
        self.arrive(self.chunk(self.i_m), 0)
        self.copy(2).start()
        self.copy(5).start()
        self.arrive(self.chunk(self.i_p), 1)
        self.copy(3).start()
        self.copy(6).start()

    def end(self):
        self.arrive(self.half_a(self.i_o), 2)
        self.arrive(self.half_b(self.i_o), 3)
        self.copy(7).start()

    def done(self):
        q = self.pos
        for k, x in ((4, q.x), (5, q.xm), (6, q.xp), (7, q.xo)):
            self.arrive(self.chunk(q.slot(x, 1 - q.c)), k)

    def drain(self):
        for k in range(8):
            self.copy(k).wait_send()


class Reduce:
    def __init__(self, pos, parts, got, relay, direct, rows, ss, rs):
        self.pos, self.parts, self.got, self.relay, self.direct = pos, parts, got, relay, direct
        self.h, self.ss, self.rs = rows // 2, ss, rs
        self.a, self.b = pl.ds(0, self.h), pl.ds(self.h, self.h)

    def pair_copy(self, x):
        q = self.pos
        return rdma(self.parts(q.slot(x, 1 - q.c)), self.got.at[x], self.ss.at[x], self.rs.at[x], q.sib)

    def x_copy(self, k):
        q, g = self.pos, self.got
        src, dst, dev = (
            lambda: (g.at[q.xo, self.a], self.relay.at[0], q.right),
            lambda: (g.at[q.xo, self.b], self.relay.at[1], q.left),
            lambda: (g.at[q.xp, self.b], self.direct.at[0, self.b], q.right),
            lambda: (g.at[q.xm, self.a], self.direct.at[1, self.a], q.left),
            lambda: (g.at[q.xp, self.a], self.direct.at[0, self.a], q.right),
            lambda: (g.at[q.xm, self.b], self.direct.at[1, self.b], q.left),
        )[k]()
        return rdma(src, dst, self.ss.at[4 + k], self.rs.at[4 + k], dev)

    def pair(self):
        for x in range(CHIPS):
            self.pair_copy(x).start()

    def first(self):
        q, g = self.pos, self.got
        for x in range(CHIPS):
            self.pair_copy(x).wait_recv()
        for n, x in enumerate((q.xo, q.xp, q.xm, q.x)):
            g[x] = g[x] + self.parts(q.slot(x, q.c))[...]
            if n == 0:
                self.x_copy(0).start()
                self.x_copy(1).start()
            elif n < 3:
                self.x_copy(n + 1).start()

    def second(self):
        q, g = self.pos, self.got
        self.x_copy(0).wait_recv()
        g[q.xp, self.a] = g[q.xp, self.a] + self.relay[0]
        self.x_copy(4).start()
        self.x_copy(1).wait_recv()
        g[q.xm, self.b] = g[q.xm, self.b] + self.relay[1]
        self.x_copy(5).start()

    def third(self):
        for k in range(2, 6):
            self.x_copy(k).wait_recv()
        return self.got[self.pos.x] + self.direct[0] + self.direct[1]

    def drain(self):
        for x in range(CHIPS):
            self.pair_copy(x).wait_send()
        for k in range(6):
            self.x_copy(k).wait_send()


def kernel(
    g_hbm, p_hbm, f_hbm, d_hbm, q_hbm, scores_ref, trail_ref, tq_ref,
    gv, pv, g3, p3, fa, ql, yq, parts, slabs,
    pan_got, pan_relay, pan_direct, got, relay, direct,
    rbuf, db, fq0, fq1, fq2, fq3, qt, xv, av, gout, acc,
    loc, ysend, yrecv, ps, pr, ms, mr, gs, gr, zs, zr,
):
    q = Place()
    fqs = [fq0, fq1, fq2, fq3]
    own = q.slot(q.x, q.c)
    source = q.z < PANELS

    loads = [
        pltpu.make_async_copy(d_hbm, db.at[own], loc.at[0]),
        pltpu.make_async_copy(q_hbm, ql, loc.at[1]),
        pltpu.make_async_copy(g_hbm, gv, loc.at[2]),
        pltpu.make_async_copy(p_hbm, pv, loc.at[3]),
        pltpu.make_async_copy(f_hbm, fa, loc.at[4]),
    ]
    for s in loads:
        s.start()

    barrier = pltpu.get_barrier_semaphore()
    others = [{"ex": lax.rem(q.y + k, 4)} for k in (1, 2, 3)]
    for dev in [q.right, q.left, q.sib, q.above, q.below] + others:
        pl.semaphore_signal(barrier, inc=1, device_id=dev, device_id_type=MESH)
    pl.semaphore_wait(barrier, 8)

    d_gather = Gather(
        q, lambda i: db.at[i], lambda i: db.at[i, pl.ds(0, 2)], lambda i: db.at[i, pl.ds(2, 2)], gs.at[0], gr.at[0]
    )
    f_gather = [
        Gather(
            q,
            lambda i, b=fqs[s]: b.at[i],
            lambda i, b=fqs[s]: b.at[i, pl.ds(0, 16)],
            lambda i, b=fqs[s]: b.at[i, pl.ds(16, 16)],
            gs.at[1 + s],
            gr.at[1 + s],
        )
        for s in range(PANELS)
    ]
    r_gather = [
        Gather(
            q,
            lambda i, s=s: rbuf.at[s, i],
            lambda i, s=s: rbuf.at[s, i, pl.ds(0, 32)],
            lambda i, s=s: rbuf.at[s, i, pl.ds(32, 32)],
            gs.at[5 + s],
            gr.at[5 + s],
        )
        for s in range(PANELS)
    ]

    def chunk_of(kind, s):
        return fqs[s].at[own] if kind == 0 else rbuf.at[s, own]

    def hop_of(s):
        return lax.rem(q.z - s + RING, RING)

    def chain(kind, s, way):
        ref = chunk_of(kind, s)
        return rdma(ref, ref, zs.at[kind, s, way], zr.at[kind, s], (q.above, q.below)[way])

    def goes(s, way):
        hop = hop_of(s)
        return hop < UP if way == 0 else (hop == 0) | (hop > UP + 1)

    def chain_send(kind, s):
        for way in range(2):
            @pl.when(goes(s, way))
            def _(way=way):
                chain(kind, s, way).start()

    def chain_drain(kind, s):
        for way in range(2):
            @pl.when(goes(s, way))
            def _(way=way):
                chain(kind, s, way).wait_send()

    def gather_of(kind, s):
        return f_gather[s] if kind == 0 else r_gather[s]

    def send_own(kind):
        for s in range(PANELS):
            @pl.when(q.z == s)
            def _(s=s):
                chain_send(kind, s)
                gather_of(kind, s).start()

    def pass_on(kind, s):
        @pl.when(q.z != s)
        def _():
            chain(kind, s, 0).wait_recv()
            chain_send(kind, s)
            gather_of(kind, s).start()

    loads[0].wait()
    d_gather.start()

    loads[1].wait()

    def y_copy(k):
        return rdma(yq.at[q.y], yq.at[q.y], ysend.at[k], yrecv.at[k], others[k])

    for s in range(1, PANELS):
        @pl.when(q.z == s)
        def _(s=s):
            pltpu.make_async_copy(
                f_hbm.at[0, :, pl.ds(0, KP * s)], fqs[s].at[own, :, pl.ds(KP, KP * s)], loc.at[5]
            ).start()

    @pl.when(source)
    def _():
        mine = ql[0]
        both = jnp.concatenate([mine, mine], axis=1)
        lane = lax.broadcasted_iota(jnp.int32, both.shape, 1)
        yq[q.y] = jnp.where(lax.div(lane, 64) == lax.rem(q.y, 2), both, 0.0)
        for k in range(3):
            y_copy(k).start()

    loads[2].wait()
    for k in range(4):
        cols = pl.ds(k * 256, 256)
        hi, lo = halves(gv[:, cols])
        g3[:, cols] = hi
        g3[:, pl.ds(1024 + k * 256, 256)] = lo
        g3[:, pl.ds(2048 + k * 256, 256)] = hi
    loads[3].wait()

    def project(m):
        for h in range(2):
            w = pv[pl.ds(2 * m + h, 1024, stride=8), :]
            hi, lo = halves(w)
            lanes = pl.ds(128 * h, 128)
            p3[pl.ds(0, 1024), lanes] = hi
            p3[pl.ds(1024, 1024), lanes] = hi
            p3[pl.ds(2048, 1024), lanes] = lo
        for i in range(8):
            parts[m, i] = jnp.dot(g3[pl.ds(64 * i, 64), :], p3[...], preferred_element_type=F32)

    panel = Reduce(q, lambda i: parts.at[0, i], pan_got, pan_relay, pan_direct, 64, ps, pr)
    main = Reduce(q, lambda i: slabs.at[i], got, relay, direct, 512, ms, mr)

    project(0)
    pl.when(source)(panel.pair)

    @pl.when(source)
    def _():
        for k in range(3):
            y_copy(k).wait_recv()
        for s in range(PANELS):
            @pl.when(q.z == s)
            def _(s=s):
                fqs[s][own, :, pl.ds(0, 128)] = yq[0] + yq[1]
                fqs[s][own, :, pl.ds(128, 128)] = yq[2] + yq[3]
                if s > 0:
                    pltpu.make_async_copy(
                        f_hbm.at[0, :, pl.ds(0, KP * s)], fqs[s].at[own, :, pl.ds(KP, KP * s)], loc.at[5]
                    ).wait()

    project(1)
    pl.when(source)(panel.first)
    send_own(0)
    project(2)
    pl.when(source)(panel.second)
    d_gather.mid()
    project(3)

    @pl.when(source)
    def _():
        rbuf[q.z, own] = panel.third()
    send_own(1)

    lane = lax.broadcasted_iota(jnp.int32, (512, 128), 1)
    for h in range(2):
        cols = pl.ds(128 * h, 128)
        rounds = [parts[m, :, :, cols].reshape(512, 128) for m in range(4)]
        for k in range(4):
            slab = None
            for m in range(4):
                turn = (32 * (m - k)) % 128
                moved = pltpu.roll(rounds[m], turn, 1) if turn else rounds[m]
                slab = moved if slab is None else jnp.where(lax.div(lane, 32) == m, moved, slab)
            slabs[4 * h + k] = slab
    main.pair()
    d_gather.end()

    order = (3, 2, 1, 0)
    pass_on(0, 3)
    main.first()
    pass_on(0, 2)
    f_gather[3].mid()
    pass_on(0, 1)
    f_gather[2].mid()
    f_gather[3].end()
    main.second()
    pass_on(0, 0)
    f_gather[1].mid()
    f_gather[2].end()
    pass_on(1, 3)
    f_gather[0].mid()
    f_gather[1].end()
    pass_on(1, 2)
    f_gather[0].end()
    r_gather[3].mid()
    pass_on(1, 1)
    r_gather[2].mid()
    r_gather[3].end()
    pass_on(1, 0)
    r_gather[1].mid()
    r_gather[2].end()
    r_gather[0].mid()
    r_gather[1].end()
    r_gather[0].end()

    d_gather.done()
    for s in order:
        f_gather[s].done()
    loads[4].wait()

    def inverse(j):
        return db[:, j].reshape(KP, KP)

    def block(l, j):
        return fqs[l][:, :, pl.ds(KP * (j + 1), KP)].reshape(KP, KP)

    for s in range(PANELS):
        qt[:, pl.ds(KP * s, KP)] = jnp.transpose(fqs[s][:, :, pl.ds(0, KP)].reshape(KP, KP))
    mine = pl.ds(pl.multiple_of(32 * own, 32), 32)
    for j in range(PANELS):
        y = qt[mine, pl.ds(KP * j, KP)]
        for l in range(j):
            y = y - dot_nt(xv[:, pl.ds(KP * l, KP)], block(j, l))
        xv[:, pl.ds(KP * j, KP)] = dot_nn(y, inverse(j))
    for j in range(PANELS):
        cols = pl.ds(KP * j, KP)
        f = fa[:, :, cols]
        m_of = lax.broadcasted_iota(jnp.int32, f.shape, 0)
        f = jnp.where(m_of * RING + q.z > j, f, 0.0)
        av[pl.ds(0, 128), cols] = f.reshape(128, KP)
        av[pl.ds(128, 32), cols] = xv[:, cols]
    for j in reversed(range(PANELS)):
        cols = pl.ds(KP * j, KP)
        y = av[:, cols]
        for l in range(j + 1, PANELS):
            y = y - dot_nn(gout[:, pl.ds(KP * l, KP)], block(l, j))
        gout[:, cols] = dot_nt(y, inverse(j))

    tq = jnp.zeros((128, 64), F32)
    yrows = pl.ds(pl.multiple_of(64 * q.y, 64), 64)
    for s in range(PANELS):
        cols = pl.ds(KP * s, KP)
        tq = tq + dot_nt(gout[pl.ds(0, 128), cols], qt[yrows, cols])
    tq_ref[...] = ql[...].reshape(128, 64) - tq

    for n, s in enumerate(order):
        r_gather[s].done()
        part = dot_nt(gout[:, pl.ds(KP * s, KP)], rbuf[s].reshape(512, KP))
        acc[...] = part if n == 0 else acc[...] + part
    slab = main.third()
    trail_ref[...] = jnp.transpose(slab) - acc[pl.ds(0, 128), :]
    scores_ref[...] = acc[pl.ds(128, 32), :] * (1.0 / math.sqrt(KP * PANELS))

    for kind in range(2):
        for s in range(PANELS):
            chain_drain(kind, s)
            gather_of(kind, s).drain()
    d_gather.drain()
    main.drain()

    @pl.when(source)
    def _():
        panel.drain()
        for k in range(3):
            y_copy(k).wait_send()


def per_device(gradients, projection, factor, diag_inverse, queries):
    vm = lambda *shape: pltpu.VMEM(shape, F32)
    dma = pltpu.SemaphoreType.DMA
    any_space = pl.BlockSpec(memory_space=pl.ANY)
    vmem_space = pl.BlockSpec(memory_space=pltpu.VMEM)
    scores, trailing, trailing_queries = pl.pallas_call(
        kernel,
        out_shape=(
            jax.ShapeDtypeStruct((32, 512), F32),
            jax.ShapeDtypeStruct((128, 512), F32),
            jax.ShapeDtypeStruct((128, 64), F32),
        ),
        in_specs=[any_space] * 5,
        out_specs=(vmem_space,) * 3,
        scratch_shapes=[
            vm(512, 1024), vm(8192, 128),
            pltpu.VMEM((512, 3072), BF16), pltpu.VMEM((3072, 256), BF16),
            vm(4, 32, 1024), vm(4, 32, 64), vm(4, 32, 128),
            vm(4, 8, 64, 256), vm(8, 512, 128),
            vm(4, 64, 256), vm(2, 32, 256), vm(2, 64, 256),
            vm(4, 512, 128), vm(2, 256, 128), vm(2, 512, 128),
            vm(4, 8, 64, 256), vm(8, 4, 32, 256),
            vm(8, 32, 256), vm(8, 32, 512), vm(8, 32, 768), vm(8, 32, 1024),
            vm(256, 1024), vm(32, 1024), vm(160, 1024), vm(160, 1024), vm(160, 512),
            dma((6,)), dma((3,)), dma((3,)),
            dma((10,)), dma((10,)), dma((10,)), dma((10,)),
            dma((9, 8)), dma((9, 8)), dma((2, 4, 2)), dma((2, 4)),
        ],
        compiler_params=pltpu.CompilerParams(
            collective_id=0, has_side_effects=True, vmem_limit_bytes=60 * 1024 * 1024
        ),
    )(
        gradients,
        projection.reshape(8192, 128),
        factor.reshape(4, 32, 1024),
        diag_inverse,
        queries.reshape(4, 32, 64),
    )
    return (
        scores,
        trailing.reshape(4, 1, 32, 512),
        trailing_queries.reshape(4, 1, 32, 64),
    )


def solution(mesh):
    return jax.shard_map(
        per_device,
        mesh=mesh,
        in_specs=(
            P("ex", "param"),
            P("param", None, "feat", None),
            P(None, "feat", "param", None),
            P(None, "param", None),
            P(None, "feat", "param", "ex"),
        ),
        out_specs=(
            P("param", "ex"),
            P(None, "feat", "param", "ex"),
            P(None, "feat", "param", "ex"),
        ),
        check_vma=False,
    )
```

time: 323 us -> 103 us (0.32)
  the two profiles are of different devices: /device:TPU:1 before, /device:TPU:290 now
where the time goes in v1:
time: 103 us; the launch traced here: 102 us
  Pallas kernels  97.2 us (94%)
  local copies, waits for them, and re-layouts  4.62 us (4%)
    pallas_call x1, Pallas kernels, per_device(): pl.pallas_call(kernel, out_shape=(jax.ShapeDtypeStruct((32, 512), F32), j...  97.2 us
    unnamed x3, local copies, waits for them, and re-layouts  4.62 us

profile of v1, /device:TPU:290, one launch (start us, length us, event | category | flops | bytes accessed | tf_op | source)
XLA Modules:
  0.0 102.5 jit_solution(3898406527140390871)
XLA Ops:
  0.6 97.2 %shard_map.76 = (f32[32,512]{1,0:T(8,128)}, f32[128,512]{1,0:T(8,128)}, f32[128,64]{1,0:T(8,128)}) custom-call(f32[512,1024]{1,0:T(8,128)} %g_hbm.1, f32[8192,128]{1,0:T(8,128)} %bitcast.9, f32[4,32,1024]{2,1,0:T(8,128)} %bitcast.10, f32[4,32,256]{2,1,0:T(8,128)} %d_hbm.1, f32[4,32,64]{2,1,0:T(8,128)} %bitcast.12), custom_call_target="tpu_custom_call" | custom-call | tf_op jit(solution)/shard_map/pallas_call | solution.py:466
  97.8 1.5 %copy.13 = f32[32,512]{1,0:T(8,128)} copy(f32[32,512]{1,0:T(8,128)} %get-tuple-element.15) | data formatting | bytes 131072
  99.3 1.7 %copy.14 = f32[4,1,32,512]{3,2,1,0:T(8,128)} copy(f32[4,1,32,512]{3,2,1,0:T(8,128)} %bitcast.11) | data formatting | bytes 524288
  101.0 1.5 %copy.15 = f32[4,1,32,64]{3,2,1,0:T(8,128)} copy(f32[4,1,32,64]{3,2,1,0:T(8,128)} %bitcast.13) | data formatting | bytes 65536

commit v2 on v1

v2 whole, which is shorter than its diff:
```python
import math

import jax
import jax.numpy as jnp
from jax import lax
from jax.experimental import pallas as pl
from jax.experimental.pallas import tpu as pltpu
from jax.sharding import PartitionSpec as P

MESH = pl.DeviceIdType.MESH
F32 = jnp.float32
BF16 = jnp.bfloat16
CHIPS = 4
PANELS = 4
RING = 16
UP = 8
KP = 256


def halves(x):
    hi = x.astype(BF16)
    return hi, (x - hi.astype(F32)).astype(BF16)


def left3(x, axis):
    hi, lo = halves(x)
    return jnp.concatenate([hi, lo, hi], axis=axis)


def right3(x, axis):
    hi, lo = halves(x)
    return jnp.concatenate([hi, hi, lo], axis=axis)


def dot_nn(a, b):
    return jnp.dot(left3(a, 1), right3(b, 0), preferred_element_type=F32)


def dot_nt(a, b):
    return lax.dot_general(
        left3(a, 1), right3(b, 1), (((1,), (1,)), ((), ())), preferred_element_type=F32
    )


class Place:
    def __init__(self):
        self.p = lax.axis_index("param")
        self.z = lax.axis_index("feat")
        self.y = lax.axis_index("ex")
        self.x = lax.div(self.p, 2)
        self.c = lax.rem(self.p, 2)
        self.xp = lax.rem(self.x + 1, CHIPS)
        self.xm = lax.rem(self.x + CHIPS - 1, CHIPS)
        self.xo = lax.rem(self.x + 2, CHIPS)
        self.right = {"param": 2 * self.xp + self.c}
        self.left = {"param": 2 * self.xm + self.c}
        self.sib = {"param": 2 * self.x + 1 - self.c}
        self.front = {"ex": lax.rem(self.y + 1, 4)}
        self.back = {"ex": lax.rem(self.y + 3, 4)}
        self.above = {"feat": lax.rem(self.z + 1, RING)}
        self.below = {"feat": lax.rem(self.z + RING - 1, RING)}

    def slot(self, x, c):
        return 2 * x + c


def rdma(src, dst, ss, rs, dev):
    return pltpu.make_async_remote_copy(
        src_ref=src, dst_ref=dst, send_sem=ss, recv_sem=rs, device_id=dev, device_id_type=MESH
    )


class Ring:
    def __init__(self, me, ahead, behind, sib, chunk, half_a, half_b, other, ss, rs):
        self.me, self.m, self.p, self.o = me, lax.rem(me + 3, 4), lax.rem(me + 1, 4), lax.rem(me + 2, 4)
        self.ahead, self.behind, self.sib = ahead, behind, sib
        self.chunk, self.half_a, self.half_b, self.other = chunk, half_a, half_b, other
        self.ss, self.rs = ss, rs

    def copy(self, k):
        ref, dev = (
            lambda: (self.chunk(self.me), self.ahead),
            lambda: (self.chunk(self.me), self.behind),
            lambda: (self.half_a(self.m), self.ahead),
            lambda: (self.half_b(self.p), self.behind),
            lambda: (self.chunk(self.me), self.sib),
            lambda: (self.chunk(self.m), self.sib),
            lambda: (self.chunk(self.p), self.sib),
            lambda: (self.chunk(self.o), self.sib),
        )[k]()
        return rdma(ref, ref, self.ss.at[k], self.rs.at[k], dev)

    def send(self, k):
        if k < 4 or self.other is not None:
            self.copy(k).start()

    def arrive(self, ref, k):
        rdma(ref, ref, self.ss.at[k], self.rs.at[k], self.sib).wait_recv()

    def start(self):
        for k in (0, 1, 4):
            self.send(k)

    def mid(self):
        self.arrive(self.chunk(self.m), 0)
        self.send(2)
        self.send(5)
        self.arrive(self.chunk(self.p), 1)
        self.send(3)
        self.send(6)

    def end(self):
        self.arrive(self.half_a(self.o), 2)
        self.arrive(self.half_b(self.o), 3)
        self.send(7)

    def done(self):
        for k, n in ((4, self.me), (5, self.m), (6, self.p), (7, self.o)):
            self.arrive(self.other(n), k)

    def drain(self):
        for k in range(4 if self.other is None else 8):
            self.copy(k).wait_send()


class Reduce:
    def __init__(self, pos, parts, got, relay, direct, rows, ss, rs):
        self.pos, self.parts, self.got, self.relay, self.direct = pos, parts, got, relay, direct
        self.h, self.ss, self.rs = rows // 2, ss, rs
        self.a, self.b = pl.ds(0, self.h), pl.ds(self.h, self.h)

    def pair_copy(self, x):
        q = self.pos
        return rdma(self.parts(q.slot(x, 1 - q.c)), self.got.at[x], self.ss.at[x], self.rs.at[x], q.sib)

    def x_copy(self, k):
        q, g = self.pos, self.got
        src, dst, dev = (
            lambda: (g.at[q.xo, self.a], self.relay.at[0], q.right),
            lambda: (g.at[q.xo, self.b], self.relay.at[1], q.left),
            lambda: (g.at[q.xp, self.b], self.direct.at[0, self.b], q.right),
            lambda: (g.at[q.xm, self.a], self.direct.at[1, self.a], q.left),
            lambda: (g.at[q.xp, self.a], self.direct.at[0, self.a], q.right),
            lambda: (g.at[q.xm, self.b], self.direct.at[1, self.b], q.left),
        )[k]()
        return rdma(src, dst, self.ss.at[4 + k], self.rs.at[4 + k], dev)

    def pair(self):
        for x in range(CHIPS):
            self.pair_copy(x).start()

    def first(self):
        q, g = self.pos, self.got
        for x in range(CHIPS):
            self.pair_copy(x).wait_recv()
        for n, x in enumerate((q.xo, q.xp, q.xm, q.x)):
            g[x] = g[x] + self.parts(q.slot(x, q.c))[...]
            if n == 0:
                self.x_copy(0).start()
                self.x_copy(1).start()
            elif n < 3:
                self.x_copy(n + 1).start()

    def second(self):
        q, g = self.pos, self.got
        self.x_copy(0).wait_recv()
        g[q.xp, self.a] = g[q.xp, self.a] + self.relay[0]
        self.x_copy(4).start()
        self.x_copy(1).wait_recv()
        g[q.xm, self.b] = g[q.xm, self.b] + self.relay[1]
        self.x_copy(5).start()

    def third(self):
        for k in range(2, 6):
            self.x_copy(k).wait_recv()
        return self.got[self.pos.x] + self.direct[0] + self.direct[1]

    def drain(self):
        for x in range(CHIPS):
            self.pair_copy(x).wait_send()
        for k in range(6):
            self.x_copy(k).wait_send()


def kernel(
    g_hbm, p_hbm, f_hbm, d_hbm, q_hbm, scores_ref, trail_ref, tq_ref,
    gv, pv, g3, p3, fa, ql, parts, slabs,
    pan_got, pan_relay, pan_direct, got, relay, direct,
    rbuf, db, fq, qs, qt, xv, av, gout, acc,
    loc, ps, pr, ms, mr, gs, gr, zs, zr, fs, fr,
):
    q = Place()
    own = q.slot(q.x, q.c)
    source = q.z < PANELS

    def lanes_of(s):
        return 128 * s * (s + 1), KP * (s + 1)

    def load(k):
        return (
            lambda: pltpu.make_async_copy(g_hbm, gv, loc.at[0]),
            lambda: pltpu.make_async_copy(p_hbm, pv, loc.at[1]),
            lambda: pltpu.make_async_copy(d_hbm.at[q.y], db.at[q.c, q.x, q.y], loc.at[2]),
            lambda: pltpu.make_async_copy(q_hbm, ql, loc.at[3]),
            lambda: pltpu.make_async_copy(f_hbm, fa, loc.at[4]),
        )[k]()

    for k in range(5):
        load(k).start()

    def rows_of(s):
        at, wide = lanes_of(s)
        return pltpu.make_async_copy(
            f_hbm.at[0, pl.ds(pl.multiple_of(8 * q.y, 8), 8), pl.ds(0, KP * s)],
            fq.at[q.c, q.x, q.y, :, pl.ds(at + KP, KP * s)],
            loc.at[5],
        )

    for s in range(1, PANELS):
        @pl.when(q.z == s)
        def _(s=s):
            rows_of(s).start()

    barrier = pltpu.get_barrier_semaphore()

    def greet(dev):
        pl.semaphore_signal(barrier, inc=1, device_id=dev, device_id_type=MESH)

    for dev in [q.right, q.left, q.sib, q.front, q.back, q.above, q.below]:
        greet(dev)
    for s in range(PANELS):
        hop = lax.rem(q.z - s + RING, RING)

        @pl.when((hop > 1) & (hop < RING - 1))
        def _(s=s):
            greet({"feat": s})

    low, high = pl.ds(0, 2), pl.ds(2, 2)
    r_ring = [
        Ring(
            q.x, q.right, q.left, q.sib,
            lambda n, s=s: rbuf.at[s, q.slot(n, q.c)],
            lambda n, s=s: rbuf.at[s, q.slot(n, q.c), pl.ds(0, 32)],
            lambda n, s=s: rbuf.at[s, q.slot(n, q.c), pl.ds(32, 32)],
            lambda n, s=s: rbuf.at[s, q.slot(n, 1 - q.c)],
            gs.at[s], gr.at[s],
        )
        for s in range(PANELS)
    ]
    fx = Ring(
        q.x, q.right, q.left, q.sib,
        lambda n: fq.at[q.c, n, q.y],
        lambda n: fq.at[q.c, n, q.y, :, pl.ds(0, 1280)],
        lambda n: fq.at[q.c, n, q.y, :, pl.ds(1280, 1280)],
        None, gs.at[4], gr.at[4],
    )
    fy = Ring(
        q.y, q.front, q.back, q.sib,
        lambda n: fq.at[q.c, :, n],
        lambda n: fq.at[q.c, low, n],
        lambda n: fq.at[q.c, high, n],
        lambda n: fq.at[1 - q.c, :, n],
        gs.at[5], gr.at[5],
    )
    dx = Ring(
        q.x, q.right, q.left, q.sib,
        lambda n: db.at[q.c, n, q.y],
        lambda n: db.at[q.c, n, q.y, pl.ds(0, 16)],
        lambda n: db.at[q.c, n, q.y, pl.ds(16, 16)],
        None, gs.at[6], gr.at[6],
    )
    dy = Ring(
        q.y, q.front, q.back, q.sib,
        lambda n: db.at[q.c, :, n],
        lambda n: db.at[q.c, low, n],
        lambda n: db.at[q.c, high, n],
        lambda n: db.at[1 - q.c, :, n],
        gs.at[7], gr.at[7],
    )

    def hop_of(s):
        return lax.rem(q.z - s + RING, RING)

    def chain(s, k, way):
        ref = rbuf.at[s, own, pl.ds(16 * k, 16)]
        return rdma(ref, ref, zs.at[s, k, way], zr.at[s, k], (q.above, q.below)[way])

    def goes(s, way):
        hop = hop_of(s)
        return hop < UP if way == 0 else (hop == 0) | (hop > UP + 1)

    def chain_send(s, k):
        for way in range(2):
            @pl.when(goes(s, way))
            def _(way=way):
                chain(s, k, way).start()

    def pass_on(s):
        @pl.when(q.z != s)
        def _():
            for k in range(4):
                chain(s, k, 0).wait_recv()
                chain_send(s, k)
            r_ring[s].start()

    def row_copy(s, k):
        at, wide = lanes_of(s)
        ref = fq.at[q.c, q.x, q.y, :, pl.ds(at, wide)]
        return rdma(ref, ref, fs.at[k], fr.at[s], {"feat": lax.rem(q.z + k, RING)})

    def rows_arrive():
        for s in range(PANELS):
            @pl.when(q.z != s)
            def _(s=s):
                row_copy(s, 1).wait_recv()

    load(0).wait()
    for k in range(4):
        cols = pl.ds(k * 256, 256)
        hi, lo = halves(gv[:, cols])
        g3[:, cols] = hi
        g3[:, pl.ds(1024 + k * 256, 256)] = lo
        g3[:, pl.ds(2048 + k * 256, 256)] = hi
    load(1).wait()

    def project(m):
        for h in range(2):
            w = pv[pl.ds(2 * m + h, 1024, stride=8), :]
            hi, lo = halves(w)
            lanes = pl.ds(128 * h, 128)
            p3[pl.ds(0, 1024), lanes] = hi
            p3[pl.ds(1024, 1024), lanes] = hi
            p3[pl.ds(2048, 1024), lanes] = lo
        for i in range(8):
            parts[m, i] = jnp.dot(g3[pl.ds(64 * i, 64), :], p3[...], preferred_element_type=F32)

    panel = Reduce(q, lambda i: parts.at[0, i], pan_got, pan_relay, pan_direct, 64, ps, pr)
    main = Reduce(q, lambda i: slabs.at[i], got, relay, direct, 512, ms, mr)

    load(3).wait()
    for s in range(PANELS):
        @pl.when(q.z == s)
        def _(s=s):
            at, wide = lanes_of(s)
            mine = ql[0]
            fq[q.c, q.x, q.y, :, pl.ds(at, KP)] = jnp.concatenate(
                [mine[8 * k : 8 * k + 8] for k in range(4)], axis=1
            )
            if s > 0:
                rows_of(s).wait()

    project(0)
    pl.semaphore_wait(barrier, jnp.where(source, 5 + RING - 1, 7))
    pl.when(source)(panel.pair)
    load(2).wait()
    dx.start()
    for s in range(PANELS):
        @pl.when(q.z == s)
        def _(s=s):
            for k in (1, 15, 2, 14, 3, 13, 4, 12, 5, 11, 6, 10, 7, 9, 8):
                row_copy(s, k).start()

    project(1)
    pl.when(source)(panel.first)
    dx.mid()
    project(2)
    pl.when(source)(panel.second)
    dx.end()
    dy.start()

    near = (q.z <= PANELS) | (q.z == RING - 1)
    far = (q.z > PANELS + 2) & (q.z < RING - 3)
    between = jnp.logical_not(near | far)

    @pl.when(near)
    def _():
        rows_arrive()
        fx.start()

    project(3)

    @pl.when(source)
    def _():
        rbuf[q.z, own] = panel.third()
        for s in range(PANELS):
            @pl.when(q.z == s)
            def _(s=s):
                for k in range(4):
                    chain_send(s, k)
                r_ring[s].start()

    dy.mid()
    pl.when(near)(fx.mid)

    lane = lax.broadcasted_iota(jnp.int32, (512, 128), 1)
    for h in range(2):
        cols = pl.ds(128 * h, 128)
        rounds = [parts[m, :, :, cols].reshape(512, 128) for m in range(4)]
        for k in range(4):
            slab = None
            for m in range(4):
                turn = (32 * (m - k)) % 128
                moved = pltpu.roll(rounds[m], turn, 1) if turn else rounds[m]
                slab = moved if slab is None else jnp.where(lax.div(lane, 32) == m, moved, slab)
            slabs[4 * h + k] = slab
    main.pair()
    dy.end()

    def panels_pass():
        pass_on(3)
        pass_on(2)
        r_ring[3].mid()
        pass_on(1)
        r_ring[2].mid()
        r_ring[3].end()
        pass_on(0)
        r_ring[1].mid()
        r_ring[2].end()

    @pl.when(near)
    def _():
        fx.end()
        fy.start()
        panels_pass()
        main.first()
        fy.mid()
        main.second()

    @pl.when(between)
    def _():
        rows_arrive()
        fx.start()
        main.first()
        fx.mid()
        fx.end()
        fy.start()
        panels_pass()
        main.second()
        fy.mid()

    @pl.when(far)
    def _():
        main.first()
        rows_arrive()
        fx.start()
        main.second()
        fx.mid()
        fx.end()
        fy.start()
        panels_pass()
        fy.mid()

    r_ring[0].mid()
    r_ring[1].end()
    fy.end()
    r_ring[0].end()

    dy.done()
    fy.done()
    load(4).wait()
    places = [(i % 2, i // 2) for i in range(8)]

    def inverse(j):
        return jnp.concatenate([db[c, x, j] for c, x in places], axis=0)

    def block(l, j):
        cols = pl.ds(lanes_of(l)[0] + KP * (j + 1), KP)
        return jnp.concatenate([fq[c, x, :, :, cols].reshape(32, KP) for c, x in places], axis=0)

    for s in range(PANELS):
        cols = pl.ds(lanes_of(s)[0], KP)
        held = [fq[:, :, y, :, cols].reshape(64, KP) for y in range(4)]
        for k in range(4):
            rows = jnp.concatenate([held[y][:, 64 * k : 64 * k + 64] for y in range(4)], axis=1)
            for c in range(2):
                for x in range(CHIPS):
                    n = 8 * (4 * c + x)
                    qs[2 * x + c, k] = rows[n : n + 8]
        qt[:, pl.ds(KP * s, KP)] = jnp.transpose(qs[...].reshape(KP, KP))
    mine = pl.ds(pl.multiple_of(32 * own, 32), 32)
    for j in range(PANELS):
        y = qt[mine, pl.ds(KP * j, KP)]
        for l in range(j):
            y = y - dot_nt(xv[:, pl.ds(KP * l, KP)], block(j, l))
        xv[:, pl.ds(KP * j, KP)] = dot_nn(y, inverse(j))
    for j in range(PANELS):
        cols = pl.ds(KP * j, KP)
        f = fa[:, :, cols]
        m_of = lax.broadcasted_iota(jnp.int32, f.shape, 0)
        f = jnp.where(m_of * RING + q.z > j, f, 0.0)
        av[pl.ds(0, 128), cols] = f.reshape(128, KP)
        av[pl.ds(128, 32), cols] = xv[:, cols]
    for j in reversed(range(PANELS)):
        cols = pl.ds(KP * j, KP)
        y = av[:, cols]
        for l in range(j + 1, PANELS):
            y = y - dot_nn(gout[:, pl.ds(KP * l, KP)], block(l, j))
        gout[:, cols] = dot_nt(y, inverse(j))

    tq = jnp.zeros((128, 64), F32)
    yrows = pl.ds(pl.multiple_of(64 * q.y, 64), 64)
    for s in range(PANELS):
        cols = pl.ds(KP * s, KP)
        tq = tq + dot_nt(gout[pl.ds(0, 128), cols], qt[yrows, cols])
    tq_ref[...] = ql[...].reshape(128, 64) - tq

    for n, s in enumerate((3, 2, 1, 0)):
        r_ring[s].done()
        part = dot_nt(gout[:, pl.ds(KP * s, KP)], rbuf[s].reshape(512, KP))
        acc[...] = part if n == 0 else acc[...] + part
    slab = main.third()
    trail_ref[...] = jnp.transpose(slab) - acc[pl.ds(0, 128), :]
    scores_ref[...] = acc[pl.ds(128, 32), :] * (1.0 / math.sqrt(KP * PANELS))

    for s in range(PANELS):
        for k in range(4):
            for way in range(2):
                @pl.when(goes(s, way))
                def _(s=s, k=k, way=way):
                    chain(s, k, way).wait_send()
        r_ring[s].drain()

        @pl.when(q.z == s)
        def _(s=s):
            for k in range(1, RING):
                row_copy(s, k).wait_send()
    for ring in (fx, fy, dx, dy):
        ring.drain()
    main.drain()
    pl.when(source)(panel.drain)


def finish(scores_in, trail_in, tq_in, scores_ref, trail_ref, tq_ref):
    scores_ref[...] = scores_in[...]
    trail_ref[...] = trail_in[...]
    tq_ref[...] = tq_in[...]


def per_device(gradients, projection, factor, diag_inverse, queries):
    vm = lambda *shape: pltpu.VMEM(shape, F32)
    dma = pltpu.SemaphoreType.DMA
    any_space = pl.BlockSpec(memory_space=pl.ANY)
    vmem_space = pl.BlockSpec(memory_space=pltpu.VMEM)
    shapes = (
        jax.ShapeDtypeStruct((32, 512), F32),
        jax.ShapeDtypeStruct((128, 512), F32),
        jax.ShapeDtypeStruct((128, 64), F32),
    )
    results = pl.pallas_call(
        kernel,
        out_shape=shapes,
        in_specs=[any_space] * 5,
        out_specs=(vmem_space,) * 3,
        scratch_shapes=[
            vm(512, 1024), vm(8192, 128),
            pltpu.VMEM((512, 3072), BF16), pltpu.VMEM((3072, 256), BF16),
            vm(4, 32, 1024), vm(4, 32, 64),
            vm(4, 8, 64, 256), vm(8, 512, 128),
            vm(4, 64, 256), vm(2, 32, 256), vm(2, 64, 256),
            vm(4, 512, 128), vm(2, 256, 128), vm(2, 512, 128),
            vm(4, 8, 64, 256), vm(2, 4, 4, 32, 256), vm(2, 4, 4, 8, 2560),
            vm(8, 4, 8, 256), vm(256, 1024), vm(32, 1024), vm(160, 1024), vm(160, 1024), vm(160, 512),
            dma((6,)), dma((10,)), dma((10,)), dma((10,)), dma((10,)),
            dma((8, 8)), dma((8, 8)), dma((4, 4, 2)), dma((4, 4)), dma((16,)), dma((4,)),
        ],
        compiler_params=pltpu.CompilerParams(
            collective_id=0, has_side_effects=True, vmem_limit_bytes=60 * 1024 * 1024
        ),
    )(
        gradients,
        projection.reshape(8192, 128),
        factor.reshape(4, 32, 1024),
        diag_inverse,
        queries.reshape(4, 32, 64),
    )
    scores, trailing, trailing_queries = pl.pallas_call(
        finish, out_shape=shapes, in_specs=[vmem_space] * 3, out_specs=(vmem_space,) * 3
    )(*results)
    return (
        scores,
        trailing.reshape(4, 1, 32, 512),
        trailing_queries.reshape(4, 1, 32, 64),
    )


def solution(mesh):
    return jax.shard_map(
        per_device,
        mesh=mesh,
        in_specs=(
            P("ex", "param"),
            P("param", None, "feat", None),
            P(None, "feat", "param", None),
            P(None, "param", None),
            P(None, "feat", "param", "ex"),
        ),
        out_specs=(
            P("param", "ex"),
            P(None, "feat", "param", "ex"),
            P(None, "feat", "param", "ex"),
        ),
        check_vma=False,
    )
```

time: 103 us -> 81.6 us (0.79)
  the two profiles are of different devices: /device:TPU:290 before, /device:TPU:288 now
where the time goes in v2:
time: 81.6 us; the launch traced here: 81.4 us
  Pallas kernels  80.8 us (99%)
    pallas_call x1, Pallas kernels, per_device(): pl.pallas_call(kernel, out_shape=shapes, in_specs=[any_space] * 5, out_sp...  79.1 us
    pallas_call x1, Pallas kernels, per_device(): pl.pallas_call(finish, out_shape=shapes, in_specs=[vmem_space] * 3, out_s...  1.71 us

profile of v2, /device:TPU:288, one launch (start us, length us, event | category | flops | bytes accessed | tf_op | source)
XLA Modules:
  0.0 81.4 jit_solution(14401053988133790256)
XLA Ops:
  0.6 79.1 %shard_map.76 = (f32[32,512]{1,0:T(8,128)}, f32[128,512]{1,0:T(8,128)}, f32[128,64]{1,0:T(8,128)}) custom-call(f32[512,1024]{1,0:T(8,128)} %g_hbm.1, f32[8192,128]{1,0:T(8,128)} %bitcast.9, f32[4,32,1024]{2,1,0:T(8,128)} %bitcast.10, f32[4,32,256]{2,1,0:T(8,128)} %d_hbm.1, f32[4,32,64]{2,1,0:T(8,128)} %bitcast.11), custom_call_target="tpu_custom_call" | custom-call | tf_op jit(solution)/shard_map/pallas_call | solution.py:549
  79.7 1.7 %shard_map.77 = (f32[32,512]{1,0:T(8,128)}, f32[128,512]{1,0:T(8,128)}, f32[128,64]{1,0:T(8,128)}) custom-call(f32[32,512]{1,0:T(8,128)} %get-tuple-element.9.scores_in, f32[128,512]{1,0:T(8,128)} %get-tuple-element.10.trail_in, f32[128,64]{1,0:T(8,128)} %get-tuple-element.11.tq_in), custom_call_target="tpu_custom_call" | custom-call | tf_op jit(solution)/shard_map/pallas_call | solution.py:576

commit v3 on v2

--- a/solution.py
+++ b/solution.py
@@ -123,6 +123,18 @@
             self.copy(k).wait_send()
 
 
+class Both:
+    def __init__(self, *rings):
+        self.rings = rings
+
+    def __getattr__(self, name):
+        def step():
+            for ring in self.rings:
+                getattr(ring, name)()
+
+        return step
+
+
 class Reduce:
     def __init__(self, pos, parts, got, relay, direct, rows, ss, rs):
         self.pos, self.parts, self.got, self.relay, self.direct = pos, parts, got, relay, direct
@@ -186,15 +198,15 @@
     g_hbm, p_hbm, f_hbm, d_hbm, q_hbm, scores_ref, trail_ref, tq_ref,
     gv, pv, g3, p3, fa, ql, parts, slabs,
     pan_got, pan_relay, pan_direct, got, relay, direct,
-    rbuf, db, fq, qs, qt, xv, av, gout, acc,
-    loc, ps, pr, ms, mr, gs, gr, zs, zr, fs, fr,
+    rbuf, db, fb, qb, qs, qt, xv, av, gout, acc,
+    dn, dt, loc, ps, pr, ms, mr, gs, gr, zs, zr, fs, fr,
 ):
     q = Place()
     own = q.slot(q.x, q.c)
     source = q.z < PANELS
 
-    def lanes_of(s):
-        return 128 * s * (s + 1), KP * (s + 1)
+    def lane_of(s):
+        return 128 * s * (s - 1)
 
     def load(k):
         return (
@@ -209,10 +221,9 @@
         load(k).start()
 
     def rows_of(s):
-        at, wide = lanes_of(s)
         return pltpu.make_async_copy(
             f_hbm.at[0, pl.ds(pl.multiple_of(8 * q.y, 8), 8), pl.ds(0, KP * s)],
-            fq.at[q.c, q.x, q.y, :, pl.ds(at + KP, KP * s)],
+            fb.at[q.c, q.x, q.y, :, pl.ds(lane_of(s), KP * s)],
             loc.at[5],
         )
 
@@ -228,13 +239,6 @@
 
     for dev in [q.right, q.left, q.sib, q.front, q.back, q.above, q.below]:
         greet(dev)
-    for s in range(PANELS):
-        hop = lax.rem(q.z - s + RING, RING)
-
-        @pl.when((hop > 1) & (hop < RING - 1))
-        def _(s=s):
-            greet({"feat": s})
-
     low, high = pl.ds(0, 2), pl.ds(2, 2)
     r_ring = [
         Ring(
@@ -247,20 +251,39 @@
         )
         for s in range(PANELS)
     ]
-    fx = Ring(
-        q.x, q.right, q.left, q.sib,
-        lambda n: fq.at[q.c, n, q.y],
-        lambda n: fq.at[q.c, n, q.y, :, pl.ds(0, 1280)],
-        lambda n: fq.at[q.c, n, q.y, :, pl.ds(1280, 1280)],
-        None, gs.at[4], gr.at[4],
-    )
-    fy = Ring(
-        q.y, q.front, q.back, q.sib,
-        lambda n: fq.at[q.c, :, n],
-        lambda n: fq.at[q.c, low, n],
-        lambda n: fq.at[q.c, high, n],
-        lambda n: fq.at[1 - q.c, :, n],
-        gs.at[5], gr.at[5],
+    fx = Both(
+        Ring(
+            q.x, q.right, q.left, q.sib,
+            lambda n: fb.at[q.c, n, q.y],
+            lambda n: fb.at[q.c, n, q.y, :, pl.ds(0, 768)],
+            lambda n: fb.at[q.c, n, q.y, :, pl.ds(768, 768)],
+            None, gs.at[4], gr.at[4],
+        ),
+        Ring(
+            q.y, q.front, q.back, q.sib,
+            lambda n: qb.at[q.c, q.x, n],
+            lambda n: qb.at[q.c, q.x, n, :, pl.ds(0, 512)],
+            lambda n: qb.at[q.c, q.x, n, :, pl.ds(512, 512)],
+            None, gs.at[8], gr.at[8],
+        ),
+    )
+    fy = Both(
+        Ring(
+            q.y, q.front, q.back, q.sib,
+            lambda n: fb.at[q.c, :, n],
+            lambda n: fb.at[q.c, low, n],
+            lambda n: fb.at[q.c, high, n],
+            lambda n: fb.at[1 - q.c, :, n],
+            gs.at[5], gr.at[5],
+        ),
+        Ring(
+            q.x, q.right, q.left, q.sib,
+            lambda n: qb.at[q.c, n],
+            lambda n: qb.at[q.c, n, low],
+            lambda n: qb.at[q.c, n, high],
+            lambda n: qb.at[1 - q.c, n],
+            gs.at[9], gr.at[9],
+        ),
     )
     dx = Ring(
         q.x, q.right, q.left, q.sib,
@@ -301,18 +324,31 @@
             for k in range(4):
                 chain(s, k, 0).wait_recv()
                 chain_send(s, k)
-            r_ring[s].start()
-
-    def row_copy(s, k):
-        at, wide = lanes_of(s)
-        ref = fq.at[q.c, q.x, q.y, :, pl.ds(at, wide)]
-        return rdma(ref, ref, fs.at[k], fr.at[s], {"feat": lax.rem(q.z + k, RING)})
-
-    def rows_arrive():
+
+    def row_copy(s, way, part):
+        if part == 0:
+            ref = qb.at[q.c, q.x, q.y, :, pl.ds(KP * s, KP)]
+        else:
+            ref = fb.at[q.c, q.x, q.y, :, pl.ds(lane_of(s), KP * s)]
+        return rdma(ref, ref, fs.at[s, way, part], fr.at[s, part], (q.above, q.below)[way])
+
+    def parts_of(s):
+        return range(1 if s == 0 else 2)
+
+    def row_send(s):
+        for way in range(2):
+            @pl.when(goes(s, way))
+            def _(way=way):
+                for part in parts_of(s):
+                    row_copy(s, way, part).start()
+
+    def rows_hop(t):
         for s in range(PANELS):
-            @pl.when(q.z != s)
+            @pl.when((hop_of(s) == t) | ((hop_of(s) == RING - t) & (t < UP)))
             def _(s=s):
-                row_copy(s, 1).wait_recv()
+                for part in parts_of(s):
+                    row_copy(s, 0, part).wait_recv()
+                row_send(s)
 
     load(0).wait()
     for k in range(4):
@@ -321,6 +357,23 @@
         g3[:, cols] = hi
         g3[:, pl.ds(1024 + k * 256, 256)] = lo
         g3[:, pl.ds(2048 + k * 256, 256)] = hi
+    load(3).wait()
+    for s in range(PANELS):
+        @pl.when(q.z == s)
+        def _(s=s):
+            mine = ql[0]
+            qb[q.c, q.x, q.y, :, pl.ds(KP * s, KP)] = jnp.concatenate(
+                [mine[8 * k : 8 * k + 8] for k in range(4)], axis=1
+            )
+            if s > 0:
+                rows_of(s).wait()
+    load(2).wait()
+    pl.semaphore_wait(barrier, 7)
+    for s in range(PANELS):
+        @pl.when(q.z == s)
+        def _(s=s):
+            row_send(s)
+    dx.start()
     load(1).wait()
 
     def project(m):
@@ -331,51 +384,42 @@
             p3[pl.ds(0, 1024), lanes] = hi
             p3[pl.ds(1024, 1024), lanes] = hi
             p3[pl.ds(2048, 1024), lanes] = lo
-        for i in range(8):
-            parts[m, i] = jnp.dot(g3[pl.ds(64 * i, 64), :], p3[...], preferred_element_type=F32)
+        parts[m] = jnp.dot(g3[...], p3[...], preferred_element_type=F32).reshape(8, 64, 256)
 
     panel = Reduce(q, lambda i: parts.at[0, i], pan_got, pan_relay, pan_direct, 64, ps, pr)
     main = Reduce(q, lambda i: slabs.at[i], got, relay, direct, 512, ms, mr)
 
-    load(3).wait()
-    for s in range(PANELS):
-        @pl.when(q.z == s)
-        def _(s=s):
-            at, wide = lanes_of(s)
-            mine = ql[0]
-            fq[q.c, q.x, q.y, :, pl.ds(at, KP)] = jnp.concatenate(
-                [mine[8 * k : 8 * k + 8] for k in range(4)], axis=1
-            )
-            if s > 0:
-                rows_of(s).wait()
+    down, upward = (0, 1, 2, 3), (3, 2, 1, 0)
+    climbs = (q.z > 1) & (q.z < UP + 2)
+
+    def sides(which):
+        return (which & climbs, upward), (which & jnp.logical_not(climbs), down)
+
+    def panels_over_x():
+        for s in upward:
+            r_ring[s].start()
 
     project(0)
-    pl.semaphore_wait(barrier, jnp.where(source, 5 + RING - 1, 7))
     pl.when(source)(panel.pair)
-    load(2).wait()
-    dx.start()
-    for s in range(PANELS):
-        @pl.when(q.z == s)
-        def _(s=s):
-            for k in (1, 15, 2, 14, 3, 13, 4, 12, 5, 11, 6, 10, 7, 9, 8):
-                row_copy(s, k).start()
-
     project(1)
     pl.when(source)(panel.first)
-    dx.mid()
+
+    @pl.when(jnp.logical_not(source))
+    def _():
+        rows_hop(1)
+
     project(2)
-    pl.when(source)(panel.second)
-    dx.end()
-    dy.start()
-
-    near = (q.z <= PANELS) | (q.z == RING - 1)
-    far = (q.z > PANELS + 2) & (q.z < RING - 3)
-    between = jnp.logical_not(near | far)
-
-    @pl.when(near)
+
+    @pl.when(source)
     def _():
-        rows_arrive()
-        fx.start()
+        rows_hop(1)
+        panel.second()
+        rows_hop(2)
+
+    @pl.when(jnp.logical_not(source))
+    def _():
+        rows_hop(2)
+        dx.mid()
 
     project(3)
 
@@ -387,10 +431,21 @@
             def _(s=s):
                 for k in range(4):
                     chain_send(s, k)
-                r_ring[s].start()
-
-    dy.mid()
-    pl.when(near)(fx.mid)
+        dx.mid()
+
+    rows_hop(3)
+
+    for side, order in sides(source):
+        @pl.when(side)
+        def _(order=order):
+            fx.start()
+            pass_on(order[0])
+            pass_on(order[1])
+            dx.end()
+            dy.start()
+            pass_on(order[2])
+            pass_on(order[3])
+            fx.mid()
 
     lane = lax.broadcasted_iota(jnp.int32, (512, 128), 1)
     for h in range(2):
@@ -404,72 +459,128 @@
                 slab = moved if slab is None else jnp.where(lax.div(lane, 32) == m, moved, slab)
             slabs[4 * h + k] = slab
     main.pair()
-    dy.end()
-
-    def panels_pass():
-        pass_on(3)
-        pass_on(2)
-        r_ring[3].mid()
-        pass_on(1)
-        r_ring[2].mid()
-        r_ring[3].end()
-        pass_on(0)
-        r_ring[1].mid()
-        r_ring[2].end()
-
-    @pl.when(near)
+    rows_hop(4)
+
+    @pl.when(jnp.logical_not(source))
+    def _():
+        dx.end()
+        dy.start()
+
+    near = (q.z == PANELS) | (q.z == RING - 1)
+    between = ((q.z > PANELS) & (q.z < PANELS + 3)) | ((q.z > RING - 4) & (q.z < RING - 1))
+    late = (q.z == PANELS + 3) | (q.z == RING - 4)
+    far = (q.z > PANELS + 3) & (q.z < RING - 4)
+
+    @pl.when(source)
     def _():
         fx.end()
         fy.start()
-        panels_pass()
         main.first()
-        fy.mid()
+        panels_over_x()
+        dy.mid()
         main.second()
-
-    @pl.when(between)
-    def _():
-        rows_arrive()
-        fx.start()
-        main.first()
-        fx.mid()
-        fx.end()
-        fy.start()
-        panels_pass()
-        main.second()
-        fy.mid()
-
-    @pl.when(far)
-    def _():
-        main.first()
-        rows_arrive()
-        fx.start()
-        main.second()
-        fx.mid()
-        fx.end()
-        fy.start()
-        panels_pass()
-        fy.mid()
-
-    r_ring[0].mid()
-    r_ring[1].end()
-    fy.end()
-    r_ring[0].end()
-
+        dy.end()
+
+    for side, order in sides(near):
+        @pl.when(side)
+        def _(order=order):
+            fx.start()
+            pass_on(order[0])
+            pass_on(order[1])
+            fx.mid()
+            main.first()
+            pass_on(order[2])
+            fx.end()
+            fy.start()
+            pass_on(order[3])
+            dy.mid()
+            panels_over_x()
+            main.second()
+            dy.end()
+
+    for side, order in sides(between):
+        @pl.when(side)
+        def _(order=order):
+            main.first()
+            rows_hop(5)
+            rows_hop(6)
+            fx.start()
+            pass_on(order[0])
+            pass_on(order[1])
+            fx.mid()
+            pass_on(order[2])
+            fx.end()
+            fy.start()
+            pass_on(order[3])
+            main.second()
+            panels_over_x()
+            dy.mid()
+            dy.end()
+
+    for side, order in sides(late):
+        @pl.when(side)
+        def _(order=order):
+            main.first()
+            rows_hop(5)
+            dy.mid()
+            rows_hop(6)
+            rows_hop(7)
+            fx.start()
+            pass_on(order[0])
+            pass_on(order[1])
+            main.second()
+            fx.mid()
+            pass_on(order[2])
+            fx.end()
+            fy.start()
+            pass_on(order[3])
+            panels_over_x()
+            dy.end()
+
+    for side, order in sides(far):
+        @pl.when(side)
+        def _(order=order):
+            main.first()
+            rows_hop(5)
+            dy.mid()
+            rows_hop(6)
+            dy.end()
+            main.second()
+            rows_hop(7)
+            pass_on(order[0])
+            rows_hop(8)
+            fx.start()
+            pass_on(order[1])
+            fx.mid()
+            pass_on(order[2])
+            fx.end()
+            fy.start()
+            pass_on(order[3])
+            panels_over_x()
+
+    for s in (3, 2, 1, 0):
+        r_ring[s].mid()
+    fy.mid()
+    for s in (3, 2, 1, 0):
+        r_ring[s].end()
     dy.done()
-    fy.done()
     load(4).wait()
     places = [(i % 2, i // 2) for i in range(8)]
-
-    def inverse(j):
-        return jnp.concatenate([db[c, x, j] for c, x in places], axis=0)
+    for j in range(PANELS):
+        inverse = jnp.concatenate([db[c, x, j] for c, x in places], axis=0)
+        dn[j] = right3(inverse, 0)
+        dt[j] = right3(inverse, 1)
+    fy.end()
+
+    fy.done()
 
     def block(l, j):
-        cols = pl.ds(lanes_of(l)[0] + KP * (j + 1), KP)
-        return jnp.concatenate([fq[c, x, :, :, cols].reshape(32, KP) for c, x in places], axis=0)
+        cols = pl.ds(lane_of(l) + KP * j, KP)
+        return jnp.concatenate([fb[c, x, :, :, cols].reshape(32, KP) for c, x in places], axis=0)
 
     for s in range(PANELS):
-        cols = pl.ds(lanes_of(s)[0], KP)
-        held = [fq[:, :, y, :, cols].reshape(64, KP) for y in range(4)]
+        cols = pl.ds(KP * s, KP)
+        held = [qb[:, :, y, :, cols].reshape(64, KP) for y in range(4)]
         for k in range(4):
             rows = jnp.concatenate([held[y][:, 64 * k : 64 * k + 64] for y in range(4)], axis=1)
             for c in range(2):
@@ -482,7 +593,7 @@
         y = qt[mine, pl.ds(KP * j, KP)]
         for l in range(j):
             y = y - dot_nt(xv[:, pl.ds(KP * l, KP)], block(j, l))
-        xv[:, pl.ds(KP * j, KP)] = dot_nn(y, inverse(j))
+        xv[:, pl.ds(KP * j, KP)] = jnp.dot(left3(y, 1), dn[j], preferred_element_type=F32)
     for j in range(PANELS):
         cols = pl.ds(KP * j, KP)
         f = fa[:, :, cols]
@@ -495,7 +606,9 @@
         y = av[:, cols]
         for l in range(j + 1, PANELS):
             y = y - dot_nn(gout[:, pl.ds(KP * l, KP)], block(l, j))
-        gout[:, cols] = dot_nt(y, inverse(j))
+        gout[:, cols] = lax.dot_general(
+            left3(y, 1), dt[j], (((1,), (1,)), ((), ())), preferred_element_type=F32
+        )
 
     tq = jnp.zeros((128, 64), F32)
     yrows = pl.ds(pl.multiple_of(64 * q.y, 64), 64)
@@ -520,10 +633,11 @@
                     chain(s, k, way).wait_send()
         r_ring[s].drain()
 
-        @pl.when(q.z == s)
-        def _(s=s):
-            for k in range(1, RING):
-                row_copy(s, k).wait_send()
+        for way in range(2):
+            @pl.when(goes(s, way))
+            def _(s=s, way=way):
+                for part in parts_of(s):
+                    row_copy(s, way, part).wait_send()
     for ring in (fx, fy, dx, dy):
         ring.drain()
     main.drain()
@@ -558,10 +672,11 @@
             vm(4, 8, 64, 256), vm(8, 512, 128),
             vm(4, 64, 256), vm(2, 32, 256), vm(2, 64, 256),
             vm(4, 512, 128), vm(2, 256, 128), vm(2, 512, 128),
-            vm(4, 8, 64, 256), vm(2, 4, 4, 32, 256), vm(2, 4, 4, 8, 2560),
+            vm(4, 8, 64, 256), vm(2, 4, 4, 32, 256), vm(2, 4, 4, 8, 1536), vm(2, 4, 4, 8, 1024),
             vm(8, 4, 8, 256), vm(256, 1024), vm(32, 1024), vm(160, 1024), vm(160, 1024), vm(160, 512),
+            pltpu.VMEM((4, 768, 256), BF16), pltpu.VMEM((4, 256, 768), BF16),
             dma((6,)), dma((10,)), dma((10,)), dma((10,)), dma((10,)),
-            dma((8, 8)), dma((8, 8)), dma((4, 4, 2)), dma((4, 4)), dma((16,)), dma((4,)),
+            dma((10, 8)), dma((10, 8)), dma((4, 4, 2)), dma((4, 4)), dma((4, 2, 2)), dma((4, 2)),
         ],
         compiler_params=pltpu.CompilerParams(
             collective_id=0, has_side_effects=True, vmem_limit_bytes=60 * 1024 * 1024

time: 81.6 us -> 70.6 us (0.87)
  the two profiles are of different devices: /device:TPU:288 before, /device:TPU:1 now
where the time goes in v3:
time: 70.6 us; the launch traced here: 70.4 us
  Pallas kernels  69.7 us (99%)
    pallas_call x1, Pallas kernels, per_device(): pl.pallas_call(kernel, out_shape=shapes, in_specs=[any_space] * 5, out_sp...  68 us
    pallas_call x1, Pallas kernels, per_device(): pl.pallas_call(finish, out_shape=shapes, in_specs=[vmem_space] * 3, out_s...  1.71 us

profile of v3, /device:TPU:1, one launch (start us, length us, event | category | flops | bytes accessed | tf_op | source)
XLA Modules:
  0.0 70.4 jit_solution(7578496848061298052)
XLA Ops:
  0.6 68.0 %shard_map.76 = (f32[32,512]{1,0:T(8,128)}, f32[128,512]{1,0:T(8,128)}, f32[128,64]{1,0:T(8,128)}) custom-call(f32[512,1024]{1,0:T(8,128)} %g_hbm.1, f32[8192,128]{1,0:T(8,128)} %bitcast.9, f32[4,32,1024]{2,1,0:T(8,128)} %bitcast.10, f32[4,32,256]{2,1,0:T(8,128)} %d_hbm.1, f32[4,32,64]{2,1,0:T(8,128)} %bitcast.11), custom_call_target="tpu_custom_call" | custom-call | tf_op jit(solution)/shard_map/pallas_call | solution.py:663
  68.7 1.7 %shard_map.77 = (f32[32,512]{1,0:T(8,128)}, f32[128,512]{1,0:T(8,128)}, f32[128,64]{1,0:T(8,128)}) custom-call(f32[32,512]{1,0:T(8,128)} %get-tuple-element.9.scores_in, f32[128,512]{1,0:T(8,128)} %get-tuple-element.10.trail_in, f32[128,64]{1,0:T(8,128)} %get-tuple-element.11.tq_in), custom_call_target="tpu_custom_call" | custom-call | tf_op jit(solution)/shard_map/pallas_call | solution.py:691

commit v4 on v3

--- a/solution.py
+++ b/solution.py
@@ -395,10 +395,6 @@
     def sides(which):
         return (which & climbs, upward), (which & jnp.logical_not(climbs), down)
 
-    def panels_over_x():
-        for s in upward:
-            r_ring[s].start()
-
     project(0)
     pl.when(source)(panel.pair)
     project(1)
@@ -434,18 +430,6 @@
         dx.mid()
 
     rows_hop(3)
-
-    for side, order in sides(source):
-        @pl.when(side)
-        def _(order=order):
-            fx.start()
-            pass_on(order[0])
-            pass_on(order[1])
-            dx.end()
-            dy.start()
-            pass_on(order[2])
-            pass_on(order[3])
-            fx.mid()
 
     lane = lax.broadcasted_iota(jnp.int32, (512, 128), 1)
     for h in range(2):
@@ -459,10 +443,10 @@
                 slab = moved if slab is None else jnp.where(lax.div(lane, 32) == m, moved, slab)
             slabs[4 * h + k] = slab
     main.pair()
-    rows_hop(4)
 
     @pl.when(jnp.logical_not(source))
     def _():
+        rows_hop(4)
         dx.end()
         dy.start()
 
@@ -471,31 +455,47 @@
     late = (q.z == PANELS + 3) | (q.z == RING - 4)
     far = (q.z > PANELS + 3) & (q.z < RING - 4)
 
-    @pl.when(source)
-    def _():
-        fx.end()
-        fy.start()
-        main.first()
-        panels_over_x()
-        dy.mid()
-        main.second()
-        dy.end()
+    def over_x(s):
+        r_ring[s].start()
+
+    for side, order in sides(source):
+        @pl.when(side)
+        def _(order=order):
+            rows_hop(4)
+            fx.start()
+            pass_on(order[0])
+            pass_on(order[1])
+            main.first()
+            dx.end()
+            dy.start()
+            pass_on(order[2])
+            fx.mid()
+            pass_on(order[3])
+            fx.end()
+            fy.start()
+            for s in order:
+                over_x(s)
+            main.second()
+            dy.mid()
+            dy.end()
 
     for side, order in sides(near):
         @pl.when(side)
         def _(order=order):
             fx.start()
             pass_on(order[0])
+            main.first()
             pass_on(order[1])
             fx.mid()
-            main.first()
             pass_on(order[2])
             fx.end()
             fy.start()
+            for s in order[:3]:
+                over_x(s)
             pass_on(order[3])
+            over_x(order[3])
+            main.second()
             dy.mid()
-            panels_over_x()
-            main.second()
             dy.end()
 
     for side, order in sides(between):
@@ -506,14 +506,17 @@
             rows_hop(6)
             fx.start()
             pass_on(order[0])
+            main.second()
+            fx.mid()
             pass_on(order[1])
-            fx.mid()
-            pass_on(order[2])
             fx.end()
             fy.start()
+            for s in order[:2]:
+                over_x(s)
+            pass_on(order[2])
+            over_x(order[2])
             pass_on(order[3])
-            main.second()
-            panels_over_x()
+            over_x(order[3])
             dy.mid()
             dy.end()
 
@@ -524,17 +527,20 @@
             rows_hop(5)
             dy.mid()
             rows_hop(6)
+            main.second()
             rows_hop(7)
             fx.start()
             pass_on(order[0])
+            fx.mid()
             pass_on(order[1])
-            main.second()
-            fx.mid()
-            pass_on(order[2])
             fx.end()
             fy.start()
+            for s in order[:2]:
+                over_x(s)
+            pass_on(order[2])
+            over_x(order[2])
             pass_on(order[3])
-            panels_over_x()
+            over_x(order[3])
             dy.end()
 
     for side, order in sides(far):
@@ -547,22 +553,34 @@
             dy.end()
             main.second()
             rows_hop(7)
-            pass_on(order[0])
             rows_hop(8)
             fx.start()
+            if order is down:
+                fx.mid()
+            pass_on(order[0])
+            if order is down:
+                fx.end()
+                fy.start()
+            else:
+                fx.mid()
             pass_on(order[1])
-            fx.mid()
+            if order is upward:
+                fx.end()
+                fy.start()
+            for s in order[:2]:
+                over_x(s)
             pass_on(order[2])
-            fx.end()
-            fy.start()
+            over_x(order[2])
             pass_on(order[3])
-            panels_over_x()
-
-    for s in (3, 2, 1, 0):
-        r_ring[s].mid()
-    fy.mid()
-    for s in (3, 2, 1, 0):
-        r_ring[s].end()
+            over_x(order[3])
+
+    for side, order in sides(q.z >= 0):
+        @pl.when(side)
+        def _(order=order):
+            for s in order:
+                r_ring[s].mid()
+            fy.mid()
+
     dy.done()
     load(4).wait()
     places = [(i % 2, i // 2) for i in range(8)]
@@ -594,6 +612,8 @@
         for l in range(j):
             y = y - dot_nt(xv[:, pl.ds(KP * l, KP)], block(j, l))
         xv[:, pl.ds(KP * j, KP)] = jnp.dot(left3(y, 1), dn[j], preferred_element_type=F32)
+    for s in upward:
+        r_ring[s].end()
     for j in range(PANELS):
         cols = pl.ds(KP * j, KP)
         f = fa[:, :, cols]

time: 70.6 us -> 67.5 us (0.956)
  the two profiles are of different devices: /device:TPU:1 before, /device:TPU:321 now
where the time goes in v4:
time: 67.5 us; the launch traced here: 67.3 us
  Pallas kernels  66.7 us (99%)
    pallas_call x1, Pallas kernels, per_device(): pl.pallas_call(kernel, out_shape=shapes, in_specs=[any_space] * 5, out_sp...  65 us
    pallas_call x1, Pallas kernels, per_device(): pl.pallas_call(finish, out_shape=shapes, in_specs=[vmem_space] * 3, out_s...  1.71 us

profile of v4, /device:TPU:321, one launch (start us, length us, event | category | flops | bytes accessed | tf_op | source)
XLA Modules:
  0.0 67.3 jit_solution(9309194112259160472)
XLA Ops:
  0.6 65.0 %shard_map.76 = (f32[32,512]{1,0:T(8,128)}, f32[128,512]{1,0:T(8,128)}, f32[128,64]{1,0:T(8,128)}) custom-call(f32[512,1024]{1,0:T(8,128)} %g_hbm.1, f32[8192,128]{1,0:T(8,128)} %bitcast.9, f32[4,32,1024]{2,1,0:T(8,128)} %bitcast.10, f32[4,32,256]{2,1,0:T(8,128)} %d_hbm.1, f32[4,32,64]{2,1,0:T(8,128)} %bitcast.11), custom_call_target="tpu_custom_call" | custom-call | tf_op jit(solution)/shard_map/pallas_call | solution.py:683
  65.6 1.7 %shard_map.77 = (f32[32,512]{1,0:T(8,128)}, f32[128,512]{1,0:T(8,128)}, f32[128,64]{1,0:T(8,128)}) custom-call(f32[32,512]{1,0:T(8,128)} %get-tuple-element.9.scores_in, f32[128,512]{1,0:T(8,128)} %get-tuple-element.10.trail_in, f32[128,64]{1,0:T(8,128)} %get-tuple-element.11.tq_in), custom_call_target="tpu_custom_call" | custom-call | tf_op jit(solution)/shard_map/pallas_call | solution.py:711

commit v5 on v4

--- a/solution.py
+++ b/solution.py
@@ -471,13 +471,12 @@
             pass_on(order[2])
             fx.mid()
             pass_on(order[3])
+            dy.mid()
             fx.end()
             fy.start()
             for s in order:
                 over_x(s)
             main.second()
-            dy.mid()
-            dy.end()
 
     for side, order in sides(near):
         @pl.when(side)
@@ -488,6 +487,7 @@
             pass_on(order[1])
             fx.mid()
             pass_on(order[2])
+            dy.mid()
             fx.end()
             fy.start()
             for s in order[:3]:
@@ -495,8 +495,6 @@
             pass_on(order[3])
             over_x(order[3])
             main.second()
-            dy.mid()
-            dy.end()
 
     for side, order in sides(between):
         @pl.when(side)
@@ -504,6 +502,7 @@
             main.first()
             rows_hop(5)
             rows_hop(6)
+            dy.mid()
             fx.start()
             pass_on(order[0])
             main.second()
@@ -517,18 +516,16 @@
             over_x(order[2])
             pass_on(order[3])
             over_x(order[3])
-            dy.mid()
-            dy.end()
 
     for side, order in sides(late):
         @pl.when(side)
         def _(order=order):
             main.first()
             rows_hop(5)
-            dy.mid()
             rows_hop(6)
             main.second()
             rows_hop(7)
+            dy.mid()
             fx.start()
             pass_on(order[0])
             fx.mid()
@@ -541,32 +538,23 @@
             over_x(order[2])
             pass_on(order[3])
             over_x(order[3])
-            dy.end()
 
     for side, order in sides(far):
         @pl.when(side)
         def _(order=order):
             main.first()
             rows_hop(5)
-            dy.mid()
             rows_hop(6)
-            dy.end()
             main.second()
             rows_hop(7)
             rows_hop(8)
+            dy.mid()
             fx.start()
-            if order is down:
-                fx.mid()
             pass_on(order[0])
-            if order is down:
-                fx.end()
-                fy.start()
-            else:
-                fx.mid()
+            fx.mid()
             pass_on(order[1])
-            if order is upward:
-                fx.end()
-                fy.start()
+            fx.end()
+            fy.start()
             for s in order[:2]:
                 over_x(s)
             pass_on(order[2])
@@ -577,9 +565,10 @@
     for side, order in sides(q.z >= 0):
         @pl.when(side)
         def _(order=order):
+            fy.mid()
+            dy.end()
             for s in order:
                 r_ring[s].mid()
-            fy.mid()
 
     dy.done()
     load(4).wait()

time: 67.5 us -> 65.8 us (0.975)
  the two profiles are of different devices: /device:TPU:321 before, /device:TPU:345 now
where the time goes in v5:
time: 65.8 us; the launch traced here: 65.6 us
  Pallas kernels  64.9 us (99%)
    pallas_call x1, Pallas kernels, per_device(): pl.pallas_call(kernel, out_shape=shapes, in_specs=[any_space] * 5, out_sp...  63.2 us
    pallas_call x1, Pallas kernels, per_device(): pl.pallas_call(finish, out_shape=shapes, in_specs=[vmem_space] * 3, out_s...  1.71 us

profile of v5, /device:TPU:345, one launch (start us, length us, event | category | flops | bytes accessed | tf_op | source)
XLA Modules:
  0.0 65.6 jit_solution(11687420788104478466)
XLA Ops:
  0.6 63.2 %shard_map.76 = (f32[32,512]{1,0:T(8,128)}, f32[128,512]{1,0:T(8,128)}, f32[128,64]{1,0:T(8,128)}) custom-call(f32[512,1024]{1,0:T(8,128)} %g_hbm.1, f32[8192,128]{1,0:T(8,128)} %bitcast.9, f32[4,32,1024]{2,1,0:T(8,128)} %bitcast.10, f32[4,32,256]{2,1,0:T(8,128)} %d_hbm.1, f32[4,32,64]{2,1,0:T(8,128)} %bitcast.11), custom_call_target="tpu_custom_call" | custom-call | tf_op jit(solution)/shard_map/pallas_call | solution.py:672
  63.9 1.7 %shard_map.77 = (f32[32,512]{1,0:T(8,128)}, f32[128,512]{1,0:T(8,128)}, f32[128,64]{1,0:T(8,128)}) custom-call(f32[32,512]{1,0:T(8,128)} %get-tuple-element.9.scores_in, f32[128,512]{1,0:T(8,128)} %get-tuple-element.10.trail_in, f32[128,64]{1,0:T(8,128)} %get-tuple-element.11.tq_in), custom_call_target="tpu_custom_call" | custom-call | tf_op jit(solution)/shard_map/pallas_call | solution.py:700
